TPU v7x, 32 devices: a whole 2x2x4 slice. The times are simulated.
32 devices in a mesh: prompt: 4 (over y, x), sample: 8 (over z, core).
Axes of the slice: x: 2, y: 2, z: 4, core: 2. Of those that a mesh axis runs over, the one named last changes fastest.
Arguments:
- queries: bfloat16 [4, 64, 4096], P('prompt', 'sample'), may hold values from -250 to 250
- prompt_cache: bfloat16 [4, 8, 2048, 2048], P('prompt', 'sample'), may hold values from -6 to 6
- owner: int32 [4], P('prompt'), may hold values from 0 to 7
- prompt_len: int32 [4], P('prompt'), may hold values from 512 to 2048
- suffix_cache: bfloat16 [4, 64, 256, 2048], P('prompt', 'sample'), may hold values from -6 to 6
- suffix_len: int32 [4, 64], P('prompt', 'sample'), may hold values from 1 to 256
- new_kv: bfloat16 [4, 64, 2048], P('prompt', 'sample'), may hold values from -6 to 6
- out_weight: bfloat16 [4096, 4096], P(None, 'sample'), may hold values from -0.09375 to 0.09375
Outputs:
- mixed: bfloat16 [4, 64, 4096], P('prompt', None, 'sample')
All inputs are finite; a program needn't handle non-finite values.
Results may differ from a plain program's by a relative error of at most 0.007.
Values may be sent and summed in bfloat16 or wider, within the bound.
A program may use at most 192 MiB of HBM per device.

v0:
```python
import jax
import jax.numpy as jnp
from jax import lax
from jax.sharding import PartitionSpec as P

H = 32
KVH = 8
HD = 128


def prefix_part(queries, cache, length):
    count = queries.shape[0]
    positions = cache.shape[0]
    query = queries.reshape(count, KVH, H // KVH, HD)
    keys = cache[:, : KVH * HD].reshape(positions, KVH, HD)
    values = cache[:, KVH * HD :].reshape(positions, KVH, HD)
    scores = jnp.einsum("sgjd,tgd->sgjt", query, keys, preferred_element_type=jnp.float32) * HD ** (
        -0.5
    )
    valid = jnp.arange(positions, dtype=jnp.int32) < length
    scores = jnp.where(valid, scores, -1e30)
    top = jnp.max(scores, axis=-1)
    weights = jnp.exp(scores - top[..., None])
    total = jnp.sum(weights, axis=-1)
    output = jnp.einsum(
        "sgjt,tgd->sgjd", weights.astype(jnp.bfloat16), values, preferred_element_type=jnp.float32
    )
    return (output.reshape(count, H, HD), top.reshape(count, H), total.reshape(count, H))


def suffix_part(queries, cache, lengths, own):
    count = queries.shape[0]
    positions = cache.shape[1]
    query = queries.reshape(count, KVH, H // KVH, HD)
    keys = cache[:, :, : KVH * HD].reshape(count, positions, KVH, HD)
    values = cache[:, :, KVH * HD :].reshape(count, positions, KVH, HD)
    own_key = own[:, : KVH * HD].reshape(count, KVH, HD)
    own_value = own[:, KVH * HD :].astype(jnp.float32).reshape(count, KVH, HD)
    scores = jnp.einsum(
        "sgjd,stgd->sgjt", query, keys, preferred_element_type=jnp.float32
    ) * HD ** (-0.5)
    valid = jnp.arange(positions, dtype=jnp.int32)[None, :] < lengths[:, None]
    scores = jnp.where(valid[:, None, None, :], scores, -1e30)
    own_score = jnp.einsum(
        "sgjd,sgd->sgj", query, own_key, preferred_element_type=jnp.float32
    ) * HD ** (-0.5)
    top = jnp.maximum(jnp.max(scores, axis=-1), own_score)
    weights = jnp.exp(scores - top[..., None])
    own_weight = jnp.exp(own_score - top)
    total = jnp.sum(weights, axis=-1) + own_weight
    output = jnp.einsum(
        "sgjt,stgd->sgjd", weights.astype(jnp.bfloat16), values, preferred_element_type=jnp.float32
    )
    own_rounded = own_weight.astype(jnp.bfloat16).astype(jnp.float32)
    output = output + own_rounded[..., None] * own_value[:, :, None, :]
    return (output.reshape(count, H, HD), top.reshape(count, H), total.reshape(count, H))


def combine(prefix, suffix):
    out_pre, top_pre, total_pre = prefix
    out_suf, top_suf, total_suf = suffix
    top = jnp.maximum(top_pre, top_suf)
    factor_pre = jnp.exp(top_pre - top)
    factor_suf = jnp.exp(top_suf - top)
    numer = out_pre * factor_pre[..., None] + out_suf * factor_suf[..., None]
    denom = total_pre * factor_pre + total_suf * factor_suf
    attn = numer / denom[..., None]
    return attn.reshape(attn.shape[0], H * HD).astype(jnp.bfloat16)


def local(queries, prompt_cache, owner, prompt_len, suffix_cache, suffix_len, new_kv, out_weight):
    local_queries = queries[0]
    length = prompt_len[0]
    holder = owner[0]
    gathered = lax.all_gather(queries, "sample", axis=1, tiled=True)
    every = gathered.shape[1]

    def compute():
        return prefix_part(gathered[0], prompt_cache[0, 0], length)

    def nothing():
        return (
            jnp.zeros((every, H, HD), jnp.float32),
            jnp.zeros((every, H), jnp.float32),
            jnp.zeros((every, H), jnp.float32),
        )

    out_all, top_all, total_all = lax.cond(lax.axis_index("sample") == holder, compute, nothing)
    out_mine, top_mine, total_mine = (
        lax.psum_scatter(out_all[None], "sample", scatter_dimension=1, tiled=True),
        lax.psum_scatter(top_all[None], "sample", scatter_dimension=1, tiled=True),
        lax.psum_scatter(total_all[None], "sample", scatter_dimension=1, tiled=True),
    )
    prefix = (out_mine[0], top_mine[0], total_mine[0])
    suffix = suffix_part(local_queries, suffix_cache[0], suffix_len[0], new_kv[0])
    attn = combine(prefix, suffix)[None]
    mixed = jnp.dot(
        lax.all_gather(attn, "sample", axis=1, tiled=True)[0],
        out_weight,
        preferred_element_type=jnp.float32,
    )[None]
    return mixed.astype(jnp.bfloat16)


def solution(mesh):
    in_specs = (
        P("prompt", "sample", None),
        P("prompt", "sample", None, None),
        P("prompt"),
        P("prompt"),
        P("prompt", "sample", None, None),
        P("prompt", "sample"),
        P("prompt", "sample", None),
        P(None, "sample"),
    )
    out_specs = P("prompt", None, "sample")
    return jax.shard_map(local, mesh=mesh, in_specs=in_specs, out_specs=out_specs, check_vma=False)
```

profile of v0, /device:TPU:7, one launch (start us, length us, event | category | flops | bytes accessed | tf_op | source)
XLA Modules:
  0.0 147.6 jit_solution(16413444352352737537)
XLA Ops:
  6.5 0.0 reduce-scatter.2.cloned.1.call-start
  7.2 15.7 %all_gather.6 = bf16[1,64,4096]{2,1,0:T(8,128)(2,1)S(1)} all-gather(bf16[1,8,4096]{2,1,0:T(8,128)(2,1)} %param.10), channel_id=1, replica_groups=mesh['prompt'=4,'sample'=8] {'sample'}, dimensions={1}, use_global_device_ids=true | all-gather | bytes 589824 | tf_op jit(solution)/shard_map/all_gather | solution.py:75
  22.9 0.0 copy-start.3
  22.9 0.0 copy-start.2
  22.9 0.0 copy-start.4
  22.9 0.0 copy-start.1
  23.0 0.8 conditional.1
  23.0 0.6 broadcast.26
  23.6 0.1 broadcast.25
  23.7 0.0 copy-start
  23.7 1.0 copy-done
  24.7 0.0 reduce-scatter.2.cloned.1.call-update
  24.8 0.0 copy-done.3
  24.8 0.1 iota_compare_fusion.1
  24.9 0.0 copy-done.2
  24.9 0.8 copy.34
  25.7 0.1 copy.42
  25.7 0.0 copy-done.4
  25.8 0.6 dynamic-slice
  27.0 0.0 copy-done.1
  27.0 0.2 fusion.19
  27.2 68.5 %all-reduce.2 = (f32[1,64,32]{2,0,1:T(1,128)S(1)}, f32[1,64,32]{2,0,1:T(1,128)S(1)}) all-reduce(f32[1,64,32]{2,0,1:T(1,128)S(1)} %bitcast.99, f32[1,64,32]{2,0,1:T(1,128)S(1)} %bitcast.100), channel_id=3, replica_groups=mesh['prompt'=4,'sample'=8] {'sample'}, use_global_device_ids=true, to_apply=%region_5.6.clone | all-reduce | flops 4096 | bytes 32768
  95.7 0.1 copy.43
  95.8 0.1 copy.35
  95.9 11.4 %copy.36 = bf16[1,8,256,2048]{2,3,1,0:T(8,128)(2,1)} copy(bf16[1,8,256,2048]{3,2,1,0:T(8,128)(2,1)} %param.14) | data formatting | bytes 16777216 | tf_op args[4]
  107.2 5.0 %fusion.31 = (bf16[8,256,1024]{1,2,0:T(8,128)(2,1)S(1)}, bf16[8,256,1024]{1,2,0:T(8,128)(2,1)}) fusion(bf16[8,256,2048]{1,2,0:T(8,128)(2,1)} %bitcast.88), kind=kLoop, calls=%fused_computation.49 | loop fusion | bytes 16777216 | tf_op jit(solution)/shard_map/slice | solution.py:35
  112.3 0.7 fusion.32
  113.0 0.1 copy.39
  113.2 0.3 fusion.13
  113.5 0.1 copy.44
  113.6 3.4 %convolution_add_fusion = f32[8,8,4,128]{3,2,1,0:T(4,128)S(1)} fusion(bf16[8,256,8,128]{1,3,2,0:T(8,128)(2,1)} %bitcast.93, f32[8,8,4,256]{3,2,1,0:T(4,128)S(1)} %get-tuple-element.50, f32[8,8,4]{2,1,0:T(8,128)S(1)} %multiply_maximum_fusion, f32[8,8,128]{2,1,0:T(8,128)S(1)} %copy.41, f32[8,8,4]{2,1,0:T(8,128)S(1)} %get-tuple-element.46), kind=kOutput, calls=%fused_computation.15 | convolution fusion | flops 16973824 | bytes 4622336 | tf_op jit(solution)/shard_map/sgjt,stgd->sgjd/dot_general | solution.py:51
  117.0 0.1 reshape.164
  117.1 0.0 reduce-scatter.2.cloned.1.call-done
  117.1 1.1 fusion.16
  118.2 18.9 %all_gather.7 = bf16[1,64,4096]{2,1,0:T(8,128)(2,1)S(1)} all-gather(bf16[1,8,4096]{2,1,0:T(8,128)(2,1)S(1)} %fusion.16), channel_id=1, replica_groups=mesh['prompt'=4,'sample'=8] {'sample'}, dimensions={1}, use_global_device_ids=true | all-gather | bytes 589824 | tf_op jit(solution)/shard_map/all_gather | solution.py:98
  137.1 3.7 %fusion.11 = bf16[1,64,512]{2,1,0:T(8,128)(2,1)} fusion(bf16[4096,512]{1,0:T(8,128)(2,1)} %param.17, bf16[1,64,4096]{2,1,0:T(8,128)(2,1)S(1)} %all_gather.7), kind=kOutput, calls=%fused_computation.17 | convolution fusion | flops 268468224 | bytes 4784128 | tf_op jit(solution)/shard_map/dot_general | solution.py:97
  (7 shorter events, 0.1 us)
Async XLA Ops:
  6.5 110.6 %reduce-scatter.2.cloned.1.call-start = ((), (), s32[]{:S(2)}) async-start(), calls=%async_computation.1 | async-start | bytes 1179648 | tf_op jit(solution)/shard_map/reduce_scatter | solution.py:90
  22.9 1.8 %copy-start.3 = (s32[1,8]{1,0:T(1,128)S(1)}, s32[1,8]{1,0:T(1,128)}, u32[]{:S(2)}) copy-start(s32[1,8]{1,0:T(1,128)} %param.15) | copy-start | bytes 100
  22.9 1.9 %copy-start.2 = (bf16[1,8,2048]{2,1,0:T(8,128)(2,1)S(1)}, bf16[1,8,2048]{2,1,0:T(8,128)(2,1)}, u32[]{:S(2)}) copy-start(bf16[1,8,2048]{2,1,0:T(8,128)(2,1)} %param.16) | copy-start | bytes 98308
  22.9 2.8 %copy-start.4 = (u32[32]{0:T(128)S(1)}, u32[32]{0:T(128)}, u32[]{:S(2)}) copy-start(u32[32]{0:T(128)} %constant.33) | copy-start | bytes 388
  22.9 4.0 %copy-start.1 = (bf16[1,8,4096]{2,1,0:T(8,128)(2,1)S(1)}, bf16[1,8,4096]{2,1,0:T(8,128)(2,1)}, u32[]{:S(2)}) copy-start(bf16[1,8,4096]{2,1,0:T(8,128)(2,1)} %param.10) | copy-start | bytes 196612
  23.7 1.0 copy-start
Sparse Core Ops, SparseCore 0:
  24.9 72.8 reduce-scatter.1
where the time goes:
time: 149 us; the launch traced here: 148 us
  blocking collectives  103 us (69%)
  local copies, waits for them, and re-layouts  20.1 us (13%)
  between operations  14.8 us (10%)
  matrix products  8 us (5%)
    unnamed x1, blocking collectives  68.5 us
    all_gather x1, blocking collectives, local(): lax.all_gather(attn, 'sample', axis=1, tiled=True)[0]  18.9 us
    all_gather x1, blocking collectives, local(): gathered = lax.all_gather(queries, 'sample', axis=1, tiled=True)  15.7 us
    unnamed x13, local copies, waits for them, and re-layouts  13 us
    slice x1, local copies, waits for them, and re-layouts, suffix_part(): keys = cache[:, :, :KVH * HD].reshape(count, positions, KVH, HD)  5.05 us
    dot_general x1, matrix products, local(): jnp.dot(lax.all_gather(attn, 'sample', axis=1, tiled=True)[0], out_weight...  3.66 us
    dot_general x1, matrix products, suffix_part(): jnp.einsum('sgjt,stgd->sgjd', weights.astype(jnp.bfloat16), values, prefe...  3.41 us
  transfers between devices with their start and end apart: 1, of which 0 were waited for; matrix products, arithmetic and copies ran while one was open for 16% of the time, Pallas kernels for 0%

commit v1 on v0

v1 whole, which is shorter than its diff:
```python
import functools

import jax
import jax.numpy as jnp
from jax import lax
from jax.experimental import pallas as pl
from jax.experimental.pallas import tpu as pltpu
from jax.sharding import PartitionSpec as P

H = 32
KVH = 8
HD = 128
GROUP = H // KVH
HALF_H = H // 2
HALF_G = KVH // 2
HALF_W = HALF_H * HD
KW = KVH * HD
GW = GROUP * HD
FACTOR = HD ** (-0.5) * 1.4426950408889634
NEG = -1e30
F32 = jnp.float32
BF16 = jnp.bfloat16
NT = (((1,), (1,)), ((), ()))


def kernel(
    n,
    owner_ref,
    plen_ref,
    slen_ref,
    q_ref,
    new_ref,
    cache_ref,
    suffix_ref,
    w_ref,
    out_ref,
    kv0,
    kv1,
    kv2,
    kv3,
    suf,
    wbuf,
    qsrc,
    qall,
    qrow,
    orow,
    ssrc,
    sall,
    stsrc,
    stall,
    mine,
    minest,
    from_left,
    from_left_st,
    from_right,
    from_right_st,
    to_right,
    to_right_st,
    to_left,
    to_left_st,
    attn,
    attn_in,
    suf_sem,
    kv_sem,
    w_sem,
    q_sem,
    q_send,
    q_recv,
    s_send,
    s_recv,
    t_send,
    t_recv,
    kv_send,
    kv_recv,
    r_send,
    r_recv,
    l_send,
    l_recv,
    a_send,
    a_recv,
):
    kv = (kv0, kv1, kv2, kv3)
    me = lax.axis_index("sample")
    chip = me // 2
    core = me % 2
    chips = n // 2
    partner = chip * 2 + (1 - core)
    count = q_ref.shape[1]
    total = n * count
    slen = suffix_ref.shape[2]

    def remote(src, dst, send, recv, to):
        return pltpu.make_async_remote_copy(
            src_ref=src,
            dst_ref=dst,
            send_sem=send,
            recv_sem=recv,
            device_id={"sample": to},
            device_id_type=pl.DeviceIdType.MESH,
        )

    suf_copies = [
        pltpu.make_async_copy(suffix_ref.at[0, b], suf.at[b], suf_sem.at[b])
        for b in range(count)
    ]
    for copy in suf_copies:
        copy.start()

    barrier = pltpu.get_barrier_semaphore()
    for d in range(1, n):
        pl.semaphore_signal(
            barrier,
            inc=1,
            device_id={"sample": (me + d) % n},
            device_id_type=pl.DeviceIdType.MESH,
        )

    q32 = q_ref[0].astype(F32)
    for half in range(2):
        qsrc[half] = q_ref[0, :, half * HALF_W : (half + 1) * HALF_W]
    for h in range(H):
        qrow[h * count : (h + 1) * count, :] = q32[:, h * HD : (h + 1) * HD]

    def kv_local(k, part):
        col = part * KW + (core * HALF_G + k) * HD
        return pltpu.make_async_copy(
            cache_ref.at[0, 0, :, pl.ds(pl.multiple_of(col, HD), HD)],
            kv[k].at[core, part],
            kv_sem.at[k, part],
        )

    def kv_remote(k, part):
        col = part * KW + ((1 - core) * HALF_G + k) * HD
        return remote(
            cache_ref.at[0, 0, :, pl.ds(pl.multiple_of(col, HD), HD)],
            kv[k].at[core, part],
            kv_send.at[k, part],
            kv_recv.at[k, part],
            partner,
        )

    def kv_arrival(k, part):
        return remote(
            kv[k].at[1 - core, part],
            kv[k].at[1 - core, part],
            kv_send.at[k, part],
            kv_recv.at[k, part],
            partner,
        )

    def w_copy(half):
        return pltpu.make_async_copy(
            w_ref.at[pl.ds(half * HALF_W, HALF_W), :], wbuf.at[half], w_sem.at[half]
        )

    pl.semaphore_wait(barrier, n - 1)

    def q_copy(d):
        to = (me + d) % n
        return remote(qsrc.at[to % 2], qall.at[me], q_send.at[d], q_recv.at[d], to)

    order = sorted(range(1, n), key=lambda d: -min(d, n - d))
    for d in order:
        q_copy(d).start()
    own_q = pltpu.make_async_copy(qsrc.at[core], qall.at[me], q_sem)
    own_q.start()
    for k in range(HALF_G):
        for part in range(2):
            kv_remote(k, part).start()
    for k in range(HALF_G):
        for part in range(2):
            kv_local(k, part).start()
    for half in range(2):
        w_copy(half).start()

    row_group = lax.broadcasted_iota(jnp.int32, (H, HD), 0) // GROUP
    lane = lax.broadcasted_iota(jnp.int32, (H, HD), 1)
    pos = lax.broadcasted_iota(jnp.int32, (1, slen), 1)
    all_m = jnp.zeros((H, HD), F32)
    all_l = jnp.zeros((H, HD), F32)
    new32 = new_ref[0].astype(F32)
    for b in range(count):
        query = qrow[pl.ds(b, H, stride=count), :]
        spread = jnp.concatenate(
            [jnp.where(row_group == g, query, 0.0) for g in range(KVH)], axis=1
        )
        own = spread * new32[b : b + 1, :KW]
        folded = own[:, :HD]
        for g in range(1, KVH):
            folded = folded + own[:, g * HD : (g + 1) * HD]
        own_score = jnp.sum(folded, axis=1, keepdims=True) * FACTOR
        suf_copies[b].wait()
        scores = lax.dot_general(
            spread.astype(BF16), suf[b, :, :KW], NT, preferred_element_type=F32
        )
        scores = jnp.where(pos < slen_ref[0, b], scores * FACTOR, NEG)
        top = jnp.maximum(jnp.max(scores, axis=1, keepdims=True), own_score)
        weights = jnp.exp2(scores - top)
        own_weight = jnp.exp2(own_score - top)
        norm = jnp.sum(weights, axis=1, keepdims=True) + own_weight
        wide = jnp.dot(
            weights.astype(BF16), suf[b, :, KW:], preferred_element_type=F32
        )
        wide = wide + own_weight.astype(BF16).astype(F32) * new32[b : b + 1, KW:]
        result = jnp.where(row_group == 0, wide[:, :HD], 0.0)
        for g in range(1, KVH):
            result = jnp.where(row_group == g, wide[:, g * HD : (g + 1) * HD], result)
        orow[pl.ds(b, H, stride=count), :] = result / norm
        all_m = jnp.where(lane == b, top, all_m)
        all_l = jnp.where(lane == b, norm, all_l)
    for h in range(H):
        half, col = h // HALF_H, (h % HALF_H) * HD
        ssrc[half, :, col : col + HD] = orow[h * count : (h + 1) * count, :].astype(BF16)
    for half in range(2):
        rows = slice(half * HALF_H, (half + 1) * HALF_H)
        block = jnp.concatenate(
            [all_m[rows], all_l[rows], jnp.zeros((HD - 2 * HALF_H, HD), F32)], axis=0
        )
        stsrc[half] = block.T[:count, :]

    def s_copy(d):
        to = (me + d) % n
        return remote(ssrc.at[to % 2], sall.at[me], s_send.at[d], s_recv.at[d], to)

    def t_copy(d):
        to = (me + d) % n
        return remote(stsrc.at[to % 2], stall.at[me], t_send.at[d], t_recv.at[d], to)

    for d in order:
        t_copy(d).start()
        s_copy(d).start()
    own_s = pltpu.make_async_copy(ssrc.at[core], sall.at[me], q_sem)
    own_t = pltpu.make_async_copy(stsrc.at[core], stall.at[me], q_sem)

    own_q.wait()
    own_s.start()
    own_s.wait()
    own_t.start()
    own_t.wait()
    for d in range(1, n):
        q_copy(d).wait_recv()

    owner = owner_ref[0]
    owner_chip = owner // 2
    slot = owner % 2
    plen = plen_ref[0]
    positions = kv0.shape[2]
    bias = jnp.where(
        lax.broadcasted_iota(jnp.int32, (1, positions), 1) < plen, 0.0, NEG
    ).astype(F32)
    wide_lane = lax.broadcasted_iota(jnp.int32, (total, HD), 1)

    last = HALF_G

    def right_copy(k):
        if isinstance(k, int) and k == last:
            src, dst = to_right_st, from_left_st
        else:
            src, dst = to_right.at[k], from_left.at[k]
        return remote(src, dst, r_send.at[k], r_recv.at[k], (me + 2) % n)

    def left_copy(k):
        if isinstance(k, int) and k == last:
            src, dst = to_left_st, from_right_st
        else:
            src, dst = to_left.at[k], from_right.at[k]
        return remote(src, dst, l_send.at[k], l_recv.at[k], (me + n - 2) % n)

    def head(k, stats):
        for part in range(2):
            kv_local(k, part).wait()
            kv_arrival(k, part).wait_recv()
        rows = [
            qall[:, :, k * GW + j * HD : k * GW + (j + 1) * HD]
            .astype(F32)
            .reshape(total, HD)
            for j in range(GROUP)
        ]
        query = jnp.concatenate(rows, axis=0).astype(BF16)
        scores = lax.dot_general(query, kv[k][slot, 0], NT, preferred_element_type=F32)
        scores = scores * FACTOR + bias
        top = jnp.max(scores, axis=1, keepdims=True)
        weights = jnp.exp2(scores - top)
        norm = jnp.sum(weights, axis=1, keepdims=True)
        result = jnp.dot(weights.astype(BF16), kv[k][slot, 1], preferred_element_type=F32)
        result = (result / norm).astype(BF16)
        block = jnp.concatenate(
            [result[j * total : (j + 1) * total] for j in range(GROUP)], axis=1
        )
        mine[k] = block
        for j in range(GROUP):
            at = k * GROUP + j
            part = slice(j * total, (j + 1) * total)
            stats = jnp.where(wide_lane == at, top[part], stats)
            stats = jnp.where(wide_lane == HALF_H + at, norm[part], stats)

        @pl.when(chip == 0)
        def _():
            to_right[k] = block
            right_copy(k).start()

        @pl.when(chip == chips - 1)
        def _():
            to_left[k] = block
            left_copy(k).start()

        return stats

    stats = jnp.zeros((total, HD), F32)
    for k in range(HALF_G):
        stats = head(k, stats)
    minest[...] = stats

    @pl.when(chip == 0)
    def _():
        to_right_st[...] = stats
        right_copy(last).start()

    @pl.when(chip == chips - 1)
    def _():
        to_left_st[...] = stats
        left_copy(last).start()

    is_mine = owner_chip == chip
    for k in range(last + 1):
        here = minest if k == last else mine.at[k]
        left_in = from_left_st if k == last else from_left.at[k]
        right_in = from_right_st if k == last else from_right.at[k]
        right_out = to_right_st if k == last else to_right.at[k]
        left_out = to_left_st if k == last else to_left.at[k]

        @pl.when(chip > 0)
        def _():
            right_copy(k).wait_recv()

        @pl.when(jnp.logical_and(chip > 0, chip < chips - 1))
        def _():
            right_out[...] = jnp.where(is_mine, here[...], left_in[...])
            right_copy(k).start()

        @pl.when(chip < chips - 1)
        def _():
            left_copy(k).wait_recv()

        @pl.when(jnp.logical_and(chip > 0, chip < chips - 1))
        def _():
            left_out[...] = jnp.where(is_mine, here[...], right_in[...])
            left_copy(k).start()

    for d in range(1, n):
        t_copy(d).wait_recv()
        s_copy(d).wait_recv()

    @pl.when(chip == 0)
    def _():
        from_left_st[...] = minest[...]
        from_left[...] = mine[...]

    @pl.when(chip == chips - 1)
    def _():
        from_right_st[...] = minest[...]
        from_right[...] = mine[...]

    before = owner_chip < chip

    def pick(own, left, right):
        return jnp.where(is_mine, own, jnp.where(before, left, right))

    pre = pick(minest[...], from_left_st[...], from_right_st[...])
    post = stall[...].reshape(total, HD)
    m_pre, l_pre = pre[:, :HALF_H], pre[:, HALF_H : 2 * HALF_H]
    m_suf, l_suf = post[:, :HALF_H], post[:, HALF_H : 2 * HALF_H]
    top = jnp.maximum(m_pre, m_suf)
    part_pre = l_pre * jnp.exp2(m_pre - top)
    part_suf = l_suf * jnp.exp2(m_suf - top)
    denom = part_pre + part_suf
    share_pre = part_pre / denom
    share_suf = part_suf / denom

    def a_copy(k):
        return remote(attn.at[k], attn_in.at[k], a_send.at[k], a_recv.at[k], partner)

    for k in range(HALF_G):
        prefix = pick(mine[k], from_left[k], from_right[k])
        for j in range(GROUP):
            h = k * GROUP + j
            cols = slice(h * HD, (h + 1) * HD)
            suffix = sall[:, :, cols].astype(F32).reshape(total, HD)
            value = (
                prefix[:, j * HD : (j + 1) * HD].astype(F32) * share_pre[:, h : h + 1]
                + suffix * share_suf[:, h : h + 1]
            )
            attn[k, :, j * HD : (j + 1) * HD] = value.astype(BF16)
        a_copy(k).start()

    for half in range(2):
        w_copy(half).wait()
    acc = jnp.zeros(out_ref.shape[1:], F32)
    for k in range(HALF_G):
        acc = acc + jnp.dot(
            attn[k], wbuf[core, k * GW : (k + 1) * GW, :], preferred_element_type=F32
        )
    for k in range(HALF_G):
        a_copy(k).wait_recv()
        acc = acc + jnp.dot(
            attn_in[k],
            wbuf[1 - core, k * GW : (k + 1) * GW, :],
            preferred_element_type=F32,
        )
    out_ref[0] = acc.astype(BF16)

    for d in range(1, n):
        q_copy(d).wait_send()
        t_copy(d).wait_send()
        s_copy(d).wait_send()
    for k in range(HALF_G):
        a_copy(k).wait_send()
        for part in range(2):
            kv_remote(k, part).wait_send()
    for k in range(last + 1):

        @pl.when(chip < chips - 1)
        def _():
            right_copy(k).wait_send()

        @pl.when(chip > 0)
        def _():
            left_copy(k).wait_send()


def local(n, queries, prompt_cache, owner, prompt_len, suffix_cache, suffix_len, new_kv, out_weight):
    count = queries.shape[1]
    total = n * count
    slen = suffix_cache.shape[2]
    positions = prompt_cache.shape[2]
    width = out_weight.shape[1]
    smem = pl.BlockSpec(memory_space=pltpu.SMEM)
    vmem = pl.BlockSpec(memory_space=pltpu.VMEM)
    hbm = pl.BlockSpec(memory_space=pltpu.HBM)
    dma = pltpu.SemaphoreType.DMA
    chunk = pltpu.VMEM((HALF_G, total, GW), BF16)
    stat = pltpu.VMEM((total, HD), F32)
    return pl.pallas_call(
        functools.partial(kernel, n),
        out_shape=jax.ShapeDtypeStruct((1, total, width), BF16),
        in_specs=[smem, smem, smem, vmem, vmem, hbm, hbm, hbm],
        out_specs=vmem,
        scratch_shapes=[
            *[pltpu.VMEM((2, 2, positions, HD), BF16)] * HALF_G,
            pltpu.VMEM((count, slen, 2 * KW), BF16),
            pltpu.VMEM((2, HALF_W, width), BF16),
            pltpu.VMEM((2, count, HALF_W), BF16),
            pltpu.VMEM((n, count, HALF_W), BF16),
            pltpu.VMEM((H * count, HD), F32),
            pltpu.VMEM((H * count, HD), F32),
            pltpu.VMEM((2, count, HALF_W), BF16),
            pltpu.VMEM((n, count, HALF_W), BF16),
            pltpu.VMEM((2, count, HD), F32),
            pltpu.VMEM((n, count, HD), F32),
            chunk,
            stat,
            chunk,
            stat,
            chunk,
            stat,
            chunk,
            stat,
            chunk,
            stat,
            chunk,
            chunk,
            dma((count,)),
            dma((HALF_G, 2)),
            dma((2,)),
            dma(()),
            dma((n,)),
            dma((n,)),
            dma((n,)),
            dma((n,)),
            dma((n,)),
            dma((n,)),
            dma((HALF_G, 2)),
            dma((HALF_G, 2)),
            dma((HALF_G + 1,)),
            dma((HALF_G + 1,)),
            dma((HALF_G + 1,)),
            dma((HALF_G + 1,)),
            dma((HALF_G,)),
            dma((HALF_G,)),
        ],
        compiler_params=pltpu.CompilerParams(
            collective_id=0, has_side_effects=True, vmem_limit_bytes=60 * 1024 * 1024
        ),
        name="shared_decode",
    )(owner, prompt_len, suffix_len, queries, new_kv, prompt_cache, suffix_cache, out_weight)


def solution(mesh):
    in_specs = (
        P("prompt", "sample", None),
        P("prompt", "sample", None, None),
        P("prompt"),
        P("prompt"),
        P("prompt", "sample", None, None),
        P("prompt", "sample"),
        P("prompt", "sample", None),
        P(None, "sample"),
    )
    out_specs = P("prompt", None, "sample")
    body = functools.partial(local, mesh.shape["sample"])
    return jax.shard_map(body, mesh=mesh, in_specs=in_specs, out_specs=out_specs, check_vma=False)
```

time: 149 us -> 62.3 us (0.42)
  the two profiles are of different devices: /device:TPU:7 before, /device:TPU:1 now
where the time goes in v1:
time: 62.3 us; the launch traced here: 62.1 us
  Pallas kernels  59.3 us (95%)
  local copies, waits for them, and re-layouts  1.47 us (2%)
  between operations  1.3 us (2%)
    pallas_call x1, Pallas kernels, local(): pl.pallas_call(functools.partial(kernel, n), out_shape=jax.ShapeDtypeStru...  59.3 us
    unnamed x1, local copies, waits for them, and re-layouts  1.47 us

profile of v1, /device:TPU:1, one launch (start us, length us, event | category | flops | bytes accessed | tf_op | source)
XLA Modules:
  0.0 62.1 jit_solution(18007691836110674968)
XLA Ops:
  1.3 59.3 %shared_decode.1 = bf16[1,64,512]{2,1,0:T(8,128)(2,1)} custom-call(s32[1]{0:T(128)S(6)} %copy.10.owner_ref, s32[1]{0:T(128)S(6)} %copy.11.plen_ref, s32[1,8]{1,0:T(1,128)} %slen_ref.1, bf16[1,8,4096]{2,1,0:T(8,128)(2,1)} %q_ref.1, bf16[1,8,2048]{2,1,0:T(8,128)(2,1)} %new_ref.1, bf16[1,1,2048,2048]{3,2,1,0:T(8,128)(2,1)} %cache_ref.1, ...), custom_call_target="tpu_custom_call" | custom-call | tf_op jit(solution)/shard_map/shared_decode/pallas_call | solution.py:443
  60.6 1.5 %copy.12 = bf16[1,64,512]{2,1,0:T(8,128)(2,1)} copy(bf16[1,64,512]{2,1,0:T(8,128)(2,1)} %shared_decode.1) | data formatting | bytes 131072

commit v2 on v1

--- a/solution.py
+++ b/solution.py
@@ -18,6 +18,7 @@
 GW = GROUP * HD
 FACTOR = HD ** (-0.5) * 1.4426950408889634
 NEG = -1e30
+HOP = 2.4
 F32 = jnp.float32
 BF16 = jnp.bfloat16
 NT = (((1,), (1,)), ((), ()))
@@ -322,30 +323,38 @@
         left_copy(last).start()
 
     is_mine = owner_chip == chip
-    for k in range(last + 1):
-        here = minest if k == last else mine.at[k]
-        left_in = from_left_st if k == last else from_left.at[k]
-        right_in = from_right_st if k == last else from_right.at[k]
-        right_out = to_right_st if k == last else to_right.at[k]
-        left_out = to_left_st if k == last else to_left.at[k]
-
-        @pl.when(chip > 0)
+    def relay_right(k, forward):
+        right_copy(k).wait_recv()
+        if forward:
+            if k == last:
+                here, came, out = minest, from_left_st, to_right_st
+            else:
+                here, came, out = mine.at[k], from_left.at[k], to_right.at[k]
+            out[...] = jnp.where(is_mine, here[...], came[...])
+            right_copy(k).start()
+
+    def relay_left(k, forward):
+        left_copy(k).wait_recv()
+        if forward:
+            if k == last:
+                here, came, out = minest, from_right_st, to_left_st
+            else:
+                here, came, out = mine.at[k], from_right.at[k], to_left.at[k]
+            out[...] = jnp.where(is_mine, here[...], came[...])
+            left_copy(k).start()
+
+    for z in range(chips):
+
+        @pl.when(chip == z)
         def _():
-            right_copy(k).wait_recv()
-
-        @pl.when(jnp.logical_and(chip > 0, chip < chips - 1))
-        def _():
-            right_out[...] = jnp.where(is_mine, here[...], left_in[...])
-            right_copy(k).start()
-
-        @pl.when(chip < chips - 1)
-        def _():
-            left_copy(k).wait_recv()
-
-        @pl.when(jnp.logical_and(chip > 0, chip < chips - 1))
-        def _():
-            left_out[...] = jnp.where(is_mine, here[...], right_in[...])
-            left_copy(k).start()
+            steps = []
+            for k in range(last + 1):
+                if z > 0:
+                    steps.append((z * HOP + k, k, relay_right, z < chips - 1))
+                if z < chips - 1:
+                    steps.append(((chips - 1 - z) * HOP + k, k, relay_left, z > 0))
+            for _, k, relay, forward in sorted(steps, key=lambda step: step[0]):
+                relay(k, forward)
 
     for d in range(1, n):
         t_copy(d).wait_recv()

time: 62.3 us -> 37.6 us (0.60)
  Pallas kernels: 59.3 us -> 34.6 us
    pallas_call x1, Pallas kernels: 59.3 us -> 34.6 us  [local(): pl.pallas_call(functools.partial(kernel, n), out_shape=jax.ShapeDtypeStru...]
where the time goes in v2:
time: 37.6 us; the launch traced here: 37.4 us
  Pallas kernels  34.6 us (92%)
  local copies, waits for them, and re-layouts  1.47 us (4%)
  between operations  1.3 us (3%)
    pallas_call x1, Pallas kernels, local(): pl.pallas_call(functools.partial(kernel, n), out_shape=jax.ShapeDtypeStru...  34.6 us
    unnamed x1, local copies, waits for them, and re-layouts  1.47 us

profile of v2, /device:TPU:1, one launch (start us, length us, event | category | flops | bytes accessed | tf_op | source)
XLA Modules:
  0.0 37.4 jit_solution(3831049732382229471)
XLA Ops:
  1.3 34.6 %shared_decode.1 = bf16[1,64,512]{2,1,0:T(8,128)(2,1)} custom-call(s32[1]{0:T(128)S(6)} %copy.10.owner_ref, s32[1]{0:T(128)S(6)} %copy.11.plen_ref, s32[1,8]{1,0:T(1,128)} %slen_ref.1, bf16[1,8,4096]{2,1,0:T(8,128)(2,1)} %q_ref.1, bf16[1,8,2048]{2,1,0:T(8,128)(2,1)} %new_ref.1, bf16[1,1,2048,2048]{3,2,1,0:T(8,128)(2,1)} %cache_ref.1, ...), custom_call_target="tpu_custom_call" | custom-call | tf_op jit(solution)/shard_map/shared_decode/pallas_call | solution.py:452
  35.9 1.5 %copy.12 = bf16[1,64,512]{2,1,0:T(8,128)(2,1)} copy(bf16[1,64,512]{2,1,0:T(8,128)(2,1)} %shared_decode.1) | data formatting | bytes 131072
